TPU v7x, 32 devices: a whole 2x2x4 slice. The times are simulated.
32 devices in a mesh: section: 2 (over y), dp: 16 (over z, x, core).
Axes of the slice: x: 2, y: 2, z: 4, core: 2. Of those that a mesh axis runs over, the one named last changes fastest.
Arguments:
- residuals: float32 [8, 128, 4096], P('section', 'dp'), may hold values from -100 to 100, as said below
- owners: int32 [32], replicated, may hold values from 0 to 31, each once
Outputs:
- harvest: bfloat16 [128, 8, 4096], P(('section', 'dp'))
Inputs may be any that keep to these rules, and one draw needn't show every extreme that they name: `owners`: a permutation of the block numbers. `residuals`: real-valued activations.
All inputs are finite; a program needn't handle non-finite values.
Results may differ from a plain program's by a relative error of at most 0.0004.
Values may be sent and summed in bfloat16 or wider, within the bound.
No kernel may reach another device: no remote copies, remote signals or barrier semaphores. Data moves between devices by JAX's collectives and lax.ppermute only.
A program may use at most 64 MiB of HBM per device.

v0:
```python
import jax
import jax.numpy as jnp
from jax import lax
from jax.sharding import PartitionSpec as P


def on_device(residuals, owners):
    layer_dev, tok_dev, features = residuals.shape
    groups = lax.axis_size("dp")
    sections = lax.axis_size("section")
    centered = residuals - jnp.mean(residuals, axis=2, keepdims=True)
    partial_value = jnp.sum(centered * centered, axis=(1, 2))
    energy = lax.psum(partial_value, "dp")
    layer_scale = 1.0 / jnp.sqrt(energy / (tok_dev * groups * features) + 1.0)
    normed = (centered * layer_scale[:, None, None]).astype(jnp.bfloat16).transpose(1, 0, 2)
    spread_rows = lax.all_to_all(normed, "dp", split_axis=2, concat_axis=0, tiled=True)
    token_total = spread_rows.shape[0]
    narrow = spread_rows.shape[2]
    blocks_all = owners.shape[0]
    block_len = token_total // blocks_all
    inverse = (
        jnp.zeros((blocks_all,), jnp.int32).at[owners].set(jnp.arange(blocks_all, dtype=jnp.int32))
    )
    ordered = spread_rows.reshape(blocks_all, block_len, layer_dev, narrow)[inverse]
    ordered = ordered.reshape(sections, groups, block_len, layer_dev, narrow)
    received = lax.all_to_all(
        lax.all_to_all(ordered, "section", split_axis=0, concat_axis=3, tiled=True),
        "dp",
        split_axis=1,
        concat_axis=4,
        tiled=True,
    )
    return received.reshape(block_len, layer_dev * sections, narrow * groups)


def solution(mesh):
    in_specs = (P("section", "dp", None), P())
    out_specs = P(("section", "dp"), None, None)
    return jax.shard_map(
        on_device, mesh=mesh, in_specs=in_specs, out_specs=out_specs, check_vma=False
    )
```

profile of v0, /device:TPU:0, one launch (start us, length us, event | category | flops | bytes accessed | tf_op | source)
XLA Modules:
  0.0 97.8 jit_solution(439982995596775943)
XLA Ops:
  0.0 1.2 %reduce_sum.18 = f32[4,8]{1,0:T(4,128)S(1)} reduce(f32[4,8,4096]{2,1,0:T(8,128)} %param.2, f32[]{:T(128)} %constant.2.clone.1), dimensions={2}, to_apply=%region_0.0 | reduce | flops 131040 | bytes 524420 | tf_op jit(solution)/shard_map/reduce_sum | solution.py:11
  1.2 1.3 %multiply_reduce_fusion = f32[4]{0:T(128)S(1)} fusion(f32[4,8,4096]{2,1,0:T(8,128)} %param.2, f32[4,8]{1,0:T(4,128)S(1)} %broadcast_multiply_fusion), kind=kLoop, calls=%fused_computation.3 | loop fusion | flops 393212 | bytes 524432 | tf_op jit(solution)/shard_map/reduce_sum | solution.py:12
  2.4 34.9 %psum.7 = f32[4]{0:T(128)S(1)} all-reduce(f32[4]{0:T(128)S(1)} %multiply_reduce_fusion), channel_id=1, replica_groups=mesh['section'=2,'dp'=16] {'dp'}, use_global_device_ids=true, to_apply=%region_2.0 | all-reduce | flops 4 | bytes 32 | tf_op jit(solution)/shard_map/psum | solution.py:13
  37.4 1.2 %fusion = bf16[8,4,4096]{2,0,1:T(8,128)(2,1)S(1)} fusion(f32[4,8,4096]{2,1,0:T(8,128)} %param.2, f32[4]{0:T(128)S(1)} %add_rsqrt_fusion, f32[4,8]{1,0:T(4,128)S(1)} %broadcast_multiply_fusion), kind=kLoop, calls=%fused_computation.4 | loop fusion | flops 393216 | bytes 786576 | tf_op jit(solution)/shard_map/transpose | solution.py:15
  38.5 0.0 copy-start
  38.5 4.6 %copy.25 = bf16[8,4,4096]{0,1,2:T(4,128)(2,1)} copy(bf16[8,4,4096]{2,0,1:T(8,128)(2,1)S(1)} %fusion) | data formatting | bytes 524288 | tf_op jit(solution)/shard_map/transpose | solution.py:15
  43.1 6.4 %reshape.39 = bf16[16,2,4096]{2,1,0:T(2,128)(2,1)} reshape(bf16[4096,4,8]{2,1,0:T(4,128)(2,1)} %bitcast.19) | data formatting | bytes 524288
  49.6 3.5 %all-to-all-start = ((bf16[16,2,4096]{2,1,0:T(2,128)(2,1)}), bf16[16,2,4096]{2,1,0:T(2,128)(2,1)S(1)}, u32[]{:S(2)}, u32[]{:S(2)}) async-start(bf16[16,2,4096]{2,1,0:T(2,128)(2,1)} %reshape.39), calls=%async_computation | async-start | bytes 524288 | tf_op jit(solution)/shard_map/all_to_all | solution.py:16
  53.1 0.0 copy-done
  53.1 0.7 scatter_custom_fusion
  53.8 9.2 %all-to-all-done = bf16[16,2,4096]{2,1,0:T(2,128)(2,1)S(1)} async-done(((bf16[16,2,4096]{2,1,0:T(2,128)(2,1)}), bf16[16,2,4096]{2,1,0:T(2,128)(2,1)S(1)}, u32[]{:S(2)}, u32[]{:S(2)}) %all-to-all-start) | async-done | bytes 262176 | tf_op jit(solution)/shard_map/all_to_all | solution.py:16
  63.1 5.9 %reshape.40 = bf16[4096,4,8]{2,1,0:T(4,128)(2,1)} reshape(bf16[16,2,4096]{2,1,0:T(2,128)(2,1)S(1)} %all-to-all-done) | data formatting | bytes 524288
  69.0 6.0 %copy.26 = bf16[8,4,16,256]{3,1,0,2:T(4,128)(2,1)S(1)} copy(bf16[8,4,16,256]{0,1,3,2:T(4,128)(2,1)} %bitcast.20) | data formatting | bytes 524288 | tf_op jit(solution)/shard_map/all_to_all | solution.py:16
  75.0 0.8 gather_fusion
  75.8 0.1 copy.28
  75.8 7.9 %all_to_all.48 = bf16[2,16,4,4,256]{4,1,3,2,0:T(8,128)(2,1)S(1)} all-to-all(bf16[2,16,4,4,256]{4,1,3,2,0:T(8,128)(2,1)S(1)} %copy.28), channel_id=1, replica_groups=mesh['section'=2,'dp'=16] {'section'}, dimensions={0} | all-to-all | bytes 524288 | tf_op jit(solution)/shard_map/all_to_all | solution.py:27
  83.8 0.1 copy.30
  83.8 13.0 %all_to_all.49 = bf16[1,16,4,8,256]{4,3,2,0,1:T(8,128)(2,1)S(1)} all-to-all(bf16[1,16,4,8,256]{4,3,2,0,1:T(8,128)(2,1)S(1)} %copy.30), channel_id=1, replica_groups=mesh['section'=2,'dp'=16] {'dp'}, dimensions={1} | all-to-all | bytes 524288 | tf_op jit(solution)/shard_map/all_to_all | solution.py:26
  96.9 0.1 copy.31
  97.0 0.8 reshape.18
  (7 shorter events, 0.0 us)
Async XLA Ops:
  38.5 14.6 %copy-start = (s32[32]{0:T(128)S(1)}, s32[32]{0:T(128)}, u32[]{:S(2)}) copy-start(s32[32]{0:T(128)} %param.3) | copy-start | bytes 388
  49.6 13.5 %all-to-all-start = ((bf16[16,2,4096]{2,1,0:T(2,128)(2,1)}), bf16[16,2,4096]{2,1,0:T(2,128)(2,1)S(1)}, u32[]{:S(2)}, u32[]{:S(2)}) async-start(bf16[16,2,4096]{2,1,0:T(2,128)(2,1)} %reshape.39), calls=%async_computation | async-start | bytes 524288 | tf_op jit(solution)/shard_map/all_to_all | solution.py:16
where the time goes:
time: 98.5 us; the launch traced here: 97.8 us
  blocking collectives  55.8 us (57%)
  local copies, waits for them, and re-layouts  25.5 us (26%)
  waiting for transfers between devices  9.24 us (9%)
  other arithmetic  3.63 us (4%)
  starting transfers between devices  3.53 us (4%)
    psum x1, blocking collectives, on_device(): energy = lax.psum(partial_value, 'dp')  34.9 us
    all_to_all x1, blocking collectives, on_device(): lax.all_to_all(lax.all_to_all(ordered, 'section', split_axis=0, concat_ax...  13 us
    unnamed x4, local copies, waits for them, and re-layouts  12.4 us
    all_to_all x1, waiting for transfers between devices, on_device(): lax.all_to_all(normed, 'dp', split_axis=2, concat_axis=0, tiled=True)  9.24 us
    all_to_all x1, blocking collectives, on_device(): lax.all_to_all(ordered, 'section', split_axis=0, concat_axis=3, tiled=True)  7.89 us
    all_to_all x1, local copies, waits for them, and re-layouts, on_device(): lax.all_to_all(normed, 'dp', split_axis=2, concat_axis=0, tiled=True)  5.97 us
    transpose x1, local copies, waits for them, and re-layouts, on_device(): (centered * layer_scale[:, None, None]).astype(jnp.bfloat16)  4.59 us
    all_to_all x1, starting transfers between devices, on_device(): lax.all_to_all(normed, 'dp', split_axis=2, concat_axis=0, tiled=True)  3.53 us
  transfers between devices with their start and end apart: 1, of which 1 were waited for; matrix products, arithmetic and copies ran while one was open for 1% of the time, Pallas kernels for 0%

commit v1 on v0

v1 whole, which is shorter than its diff:
```python
import jax
import jax.numpy as jnp
from jax import lax
from jax.experimental import pallas as pl
from jax.experimental.pallas import tpu as pltpu
from jax.sharding import PartitionSpec as P

LANES = 128
SUBLANES = 8


def spread_kernel(x_ref, out_ref):
    layer_dev, tok_dev, features = x_ref.shape
    groups = out_ref.shape[0]
    strips = features // groups // LANES
    rows = tok_dev * layer_dev
    row_layer = lax.broadcasted_iota(jnp.int32, (SUBLANES, LANES), 0) % layer_dev
    energy = jnp.zeros((SUBLANES, LANES), jnp.float32)
    for layer in range(layer_dev):
        value = x_ref[layer]
        centered = value - jnp.mean(value, axis=1, keepdims=True)
        partial_value = jnp.sum(centered * centered)
        energy = jnp.where(row_layer == layer, partial_value, energy)
        for strip in range(groups * strips):
            group, part = divmod(strip, strips)
            out_ref[group, pl.ds(part * rows + layer, tok_dev, stride=layer_dev), :] = centered[
                :, strip * LANES : (strip + 1) * LANES
            ]
    for group in range(groups):
        out_ref[group, strips * rows :, :] = energy


def route_kernel(count, block_rows, owners_ref, x_ref, out_ref):
    groups, all_rows, _ = x_ref.shape
    blocks, message_rows, _ = out_ref.shape
    strips = message_rows // block_rows
    rows = (all_rows - SUBLANES) // strips
    blocks_dev = blocks // groups
    energy = x_ref[0, strips * rows :, :]
    for group in range(1, groups):
        energy += x_ref[group, strips * rows :, :]
    scale = 1.0 / jnp.sqrt(energy / count + 1.0)
    scale = jnp.concatenate([scale] * (block_rows // SUBLANES), axis=0)
    for group in range(groups):
        for block in range(blocks_dev):
            owner = owners_ref[group * blocks_dev + block]
            for part in range(strips):
                start = part * rows + block * block_rows
                value = x_ref[group, start : start + block_rows, :] * scale
                out_ref[owner, part * block_rows : (part + 1) * block_rows, :] = value.astype(
                    jnp.bfloat16
                )


def merge_kernel(layer_dev, x_ref, out_ref):
    block_len, layers, features = out_ref.shape
    devices, message_rows, _ = x_ref.shape
    block_rows = block_len * layer_dev
    strips = message_rows // block_rows
    sections = layers // layer_dev
    groups = devices // sections
    for group in range(groups):
        for part in range(strips):
            column = (group * strips + part) * LANES
            for token in range(block_len):
                start = part * block_rows + token * layer_dev
                value = jnp.concatenate(
                    [
                        x_ref[section * groups + group, start : start + layer_dev, :]
                        for section in range(sections)
                    ],
                    axis=0,
                )
                out_ref[token, :, column : column + LANES] = value


def on_device(residuals, owners):
    layer_dev, tok_dev, features = residuals.shape
    groups = lax.axis_size("dp")
    sections = lax.axis_size("section")
    blocks = owners.shape[0]
    block_len = tok_dev * groups // blocks
    strips = features // groups // LANES
    rows = tok_dev * layer_dev
    block_rows = block_len * layer_dev
    message = pl.pallas_call(
        spread_kernel,
        out_shape=jax.ShapeDtypeStruct((groups, strips * rows + SUBLANES, LANES), jnp.float32),
        name="spread",
    )(residuals)
    spread = lax.all_to_all(message, "dp", split_axis=0, concat_axis=0, tiled=True)
    routed = pl.pallas_call(
        lambda *refs: route_kernel(float(tok_dev * groups * features), block_rows, *refs),
        out_shape=jax.ShapeDtypeStruct((blocks, strips * block_rows, LANES), jnp.bfloat16),
        in_specs=[
            pl.BlockSpec(memory_space=pltpu.SMEM),
            pl.BlockSpec(memory_space=pltpu.VMEM),
        ],
        name="route",
    )(owners, spread)
    received = lax.all_to_all(routed, ("section", "dp"), split_axis=0, concat_axis=0, tiled=True)
    return pl.pallas_call(
        lambda *refs: merge_kernel(layer_dev, *refs),
        out_shape=jax.ShapeDtypeStruct((block_len, layer_dev * sections, features), jnp.bfloat16),
        name="merge",
    )(received)


def solution(mesh):
    in_specs = (P("section", "dp", None), P())
    out_specs = P(("section", "dp"), None, None)
    return jax.shard_map(
        on_device, mesh=mesh, in_specs=in_specs, out_specs=out_specs, check_vma=False
    )
```

time: 98.5 us -> 44.4 us (0.45)
  local copies, waits for them, and re-layouts: 25.5 us -> 0 us
  blocking collectives: 55.8 us -> 38.3 us
  waiting for transfers between devices: 9.24 us -> 0 us
  Pallas kernels: 0 us -> 5.79 us
  other arithmetic: 3.63 us -> 0 us
  starting transfers between devices: 3.53 us -> 0 us
    psum x1 -> x0, blocking collectives: 34.9 us -> none  [on_device(): energy = lax.psum(partial_value, 'dp')]
    all_to_all x2, blocking collectives: 20.9 us -> 38.3 us  [the longest x1 24.7 us: on_device(): lax.all_to_all(message, 'dp', split_axis=0, concat_axis=0, tiled=True)]
    unnamed x4 -> x0, local copies, waits for them, and re-layouts: 12.4 us -> none
    all_to_all x1 -> x0, waiting for transfers between devices: 9.24 us -> none  [on_device(): lax.all_to_all(normed, 'dp', split_axis=2, concat_axis=0, tiled=True)]
    all_to_all x4 -> x0, local copies, waits for them, and re-layouts: 6.22 us -> none  [the longest x1 5.97 us: on_device(): lax.all_to_all(normed, 'dp', split_axis=2, concat_axis=0, tiled=True)]
    pallas_call x0 -> x3, Pallas kernels: none -> 5.79 us  [the longest x1 2.2 us: on_device(): pl.pallas_call(spread_kernel, out_shape=jax.ShapeDtypeStruct((groups, str...]
    transpose x1 -> x0, local copies, waits for them, and re-layouts: 4.59 us -> none  [on_device(): (centered * layer_scale[:, None, None]).astype(jnp.bfloat16)]
    all_to_all x1 -> x0, starting transfers between devices: 3.53 us -> none  [on_device(): lax.all_to_all(normed, 'dp', split_axis=2, concat_axis=0, tiled=True)]
  transfers between devices with their start and end apart: 1 -> 0, of which waited for: 1 -> 0; matrix products, arithmetic and copies ran while one was open for 1% -> 0% of each run, Pallas kernels for 0% -> 0%
where the time goes in v1:
time: 44.4 us; the launch traced here: 44.1 us
  blocking collectives  38.3 us (86%)
  Pallas kernels  5.79 us (13%)
    all_to_all x1, blocking collectives, on_device(): lax.all_to_all(message, 'dp', split_axis=0, concat_axis=0, tiled=True)  24.7 us
    all_to_all x1, blocking collectives, on_device(): lax.all_to_all(routed, ('section', 'dp'), split_axis=0, concat_axis=0, ti...  13.6 us
    pallas_call x1, Pallas kernels, on_device(): pl.pallas_call(spread_kernel, out_shape=jax.ShapeDtypeStruct((groups, str...  2.2 us
    pallas_call x1, Pallas kernels, on_device(): pl.pallas_call(lambda *refs: route_kernel(float(tok_dev * groups * featur...  1.84 us
    pallas_call x1, Pallas kernels, on_device(): pl.pallas_call(lambda *refs: merge_kernel(layer_dev, *refs), out_shape=ja...  1.75 us

profile of v1, /device:TPU:0, one launch (start us, length us, event | category | flops | bytes accessed | tf_op | source)
XLA Modules:
  0.0 44.1 jit_solution(1105296908733696434)
XLA Ops:
  0.0 2.2 %spread.1 = f32[16,72,128]{2,1,0:T(8,128)} custom-call(f32[4,8,4096]{2,1,0:T(8,128)} %x_ref.1), custom_call_target="tpu_custom_call" | custom-call | tf_op jit(solution)/shard_map/spread/pallas_call | solution.py:86
  2.2 24.7 %all_to_all.10.refs_1_ = f32[16,72,128]{2,1,0:T(8,128)} all-to-all(f32[16,72,128]{2,1,0:T(8,128)} %spread.1), channel_id=1, replica_groups=mesh['section'=2,'dp'=16] {'dp'}, dimensions={0} | all-to-all | bytes 1179648 | tf_op jit(solution)/shard_map/all_to_all | solution.py:91
  26.9 1.8 %route.1 = bf16[32,32,128]{2,1,0:T(8,128)(2,1)} custom-call(s32[32]{0:T(128)} %refs_0_.1, f32[16,72,128]{2,1,0:T(8,128)} %all_to_all.10.refs_1_), custom_call_target="tpu_custom_call" | custom-call | tf_op jit(solution)/shard_map/route/pallas_call | solution.py:92
  28.8 13.6 %all_to_all.11.refs_0_ = bf16[32,32,128]{2,1,0:T(8,128)(2,1)} all-to-all(bf16[32,32,128]{2,1,0:T(8,128)(2,1)} %route.1), channel_id=1, replica_groups=mesh['section'=2,'dp'=16] {'section','dp'}, dimensions={0} | all-to-all | bytes 524288 | tf_op jit(solution)/shard_map/all_to_all | solution.py:101
  42.3 1.8 %merge.1 = bf16[4,8,4096]{2,1,0:T(8,128)(2,1)} custom-call(bf16[32,32,128]{2,1,0:T(8,128)(2,1)} %all_to_all.11.refs_0_), custom_call_target="tpu_custom_call" | custom-call | tf_op jit(solution)/shard_map/merge/pallas_call | solution.py:102

commit v2 on v1

--- a/solution.py
+++ b/solution.py
@@ -7,6 +7,7 @@
 
 LANES = 128
 SUBLANES = 8
+LOCAL = pltpu.CompilerParams(vmem_limit_bytes=16 * 1024 * 1024)
 
 
 def spread_kernel(x_ref, out_ref):
@@ -86,6 +87,7 @@
     message = pl.pallas_call(
         spread_kernel,
         out_shape=jax.ShapeDtypeStruct((groups, strips * rows + SUBLANES, LANES), jnp.float32),
+        compiler_params=LOCAL,
         name="spread",
     )(residuals)
     spread = lax.all_to_all(message, "dp", split_axis=0, concat_axis=0, tiled=True)
@@ -96,12 +98,14 @@
             pl.BlockSpec(memory_space=pltpu.SMEM),
             pl.BlockSpec(memory_space=pltpu.VMEM),
         ],
+        compiler_params=LOCAL,
         name="route",
     )(owners, spread)
     received = lax.all_to_all(routed, ("section", "dp"), split_axis=0, concat_axis=0, tiled=True)
     return pl.pallas_call(
         lambda *refs: merge_kernel(layer_dev, *refs),
         out_shape=jax.ShapeDtypeStruct((block_len, layer_dev * sections, features), jnp.bfloat16),
+        compiler_params=LOCAL,
         name="merge",
     )(received)
 

time: 44.4 us -> 40.5 us (0.912)
  Pallas kernels: 5.79 us -> 1.76 us
  local copies, waits for them, and re-layouts: 0 us -> 1.05 us
  blocking collectives: 38.3 us -> 37.4 us
    pallas_call x1, Pallas kernels: 2.2 us -> 0.36 us  [on_device(): pl.pallas_call(spread_kernel, out_shape=jax.ShapeDtypeStruct((groups, str...]
    pallas_call x1, Pallas kernels: 1.84 us -> 0.6 us  [on_device(): pl.pallas_call(lambda *refs: route_kernel(float(tok_dev * groups * featur...]
    unnamed x0 -> x4, local copies, waits for them, and re-layouts: none -> 1.05 us
    pallas_call x1, Pallas kernels: 1.75 us -> 0.8 us  [on_device(): pl.pallas_call(lambda *refs: merge_kernel(layer_dev, *refs), out_shape=ja...]
    all_to_all x1, blocking collectives: 13.6 us -> 13 us  [on_device(): lax.all_to_all(routed, ('section', 'dp'), split_axis=0, concat_axis=0, ti...]
where the time goes in v2:
time: 40.5 us; the launch traced here: 40.3 us
  blocking collectives  37.4 us (92%)
  Pallas kernels  1.76 us (4%)
  local copies, waits for them, and re-layouts  1.05 us (3%)
    all_to_all x1, blocking collectives, on_device(): lax.all_to_all(message, 'dp', split_axis=0, concat_axis=0, tiled=True)  24.4 us
    all_to_all x1, blocking collectives, on_device(): lax.all_to_all(routed, ('section', 'dp'), split_axis=0, concat_axis=0, ti...  13 us
    unnamed x4, local copies, waits for them, and re-layouts  1.05 us

profile of v2, /device:TPU:0, one launch (start us, length us, event | category | flops | bytes accessed | tf_op | source)
XLA Modules:
  0.0 40.3 jit_solution(5649799206866920060)
XLA Ops:
  0.0 0.0 copy-start
  0.0 1.0 %copy-done = f32[4,8,4096]{2,1,0:T(8,128)S(1)} copy-done((f32[4,8,4096]{2,1,0:T(8,128)S(1)}, f32[4,8,4096]{2,1,0:T(8,128)}, u32[]{:S(2)}) %copy-start) | copy-done | bytes 524312
  1.0 0.4 spread.1
  1.4 0.0 copy-start.1
  1.4 24.4 %all_to_all.10.refs_1_ = f32[16,72,128]{2,1,0:T(8,128)S(1)} all-to-all(f32[16,72,128]{2,1,0:T(8,128)S(1)} %spread.1), channel_id=1, replica_groups=mesh['section'=2,'dp'=16] {'dp'}, dimensions={0} | all-to-all | bytes 1179648 | tf_op jit(solution)/shard_map/all_to_all | solution.py:93
  25.8 0.0 copy-done.1
  25.8 0.6 %route.1 = bf16[32,32,128]{2,1,0:T(8,128)(2,1)S(1)} custom-call(s32[32]{0:T(128)S(1)} %copy-done.1, f32[16,72,128]{2,1,0:T(8,128)S(1)} %all_to_all.10.refs_1_), custom_call_target="tpu_custom_call" | custom-call | tf_op jit(solution)/shard_map/route/pallas_call | solution.py:94
  26.4 13.0 %all_to_all.11.refs_0_ = bf16[32,32,128]{2,1,0:T(8,128)(2,1)S(1)} all-to-all(bf16[32,32,128]{2,1,0:T(8,128)(2,1)S(1)} %route.1), channel_id=1, replica_groups=mesh['section'=2,'dp'=16] {'section','dp'}, dimensions={0} | all-to-all | bytes 524288 | tf_op jit(solution)/shard_map/all_to_all | solution.py:104
  39.5 0.8 %merge.1 = bf16[4,8,4096]{2,1,0:T(8,128)(2,1)} custom-call(bf16[32,32,128]{2,1,0:T(8,128)(2,1)S(1)} %all_to_all.11.refs_0_), custom_call_target="tpu_custom_call" | custom-call | tf_op jit(solution)/shard_map/merge/pallas_call | solution.py:105
Async XLA Ops:
  0.0 1.0 %copy-start = (f32[4,8,4096]{2,1,0:T(8,128)S(1)}, f32[4,8,4096]{2,1,0:T(8,128)}, u32[]{:S(2)}) copy-start(f32[4,8,4096]{2,1,0:T(8,128)} %x_ref.1) | copy-start | bytes 1572868
  1.4 24.4 %copy-start.1 = (s32[32]{0:T(128)S(1)}, s32[32]{0:T(128)}, u32[]{:S(2)}) copy-start(s32[32]{0:T(128)} %refs_0_.1) | copy-start | bytes 388

commit v3 on v2

--- a/solution.py
+++ b/solution.py
@@ -7,50 +7,78 @@
 
 LANES = 128
 SUBLANES = 8
+PARTS = 3
 LOCAL = pltpu.CompilerParams(vmem_limit_bytes=16 * 1024 * 1024)
 
 
-def spread_kernel(x_ref, out_ref):
+def split(value):
+    high = value.astype(jnp.bfloat16)
+    return high, value - high.astype(jnp.float32)
+
+
+def energy_slots(shape, layer_dev):
+    row = lax.broadcasted_iota(jnp.int32, shape, 0)
+    lane = lax.broadcasted_iota(jnp.int32, shape, 1)
+    return row, lane, (row < layer_dev) & (lane < PARTS)
+
+
+def spread_kernel(x_ref, out_ref, rows_ref):
     layer_dev, tok_dev, features = x_ref.shape
-    groups = out_ref.shape[0]
+    groups, all_rows, _ = out_ref.shape
     strips = features // groups // LANES
     rows = tok_dev * layer_dev
-    row_layer = lax.broadcasted_iota(jnp.int32, (SUBLANES, LANES), 0) % layer_dev
-    energy = jnp.zeros((SUBLANES, LANES), jnp.float32)
+    half = all_rows // 2
+    tile = 2 * SUBLANES
+    row, lane, slots = energy_slots((tile, LANES), layer_dev)
+    energy = jnp.zeros((tile, LANES), jnp.float32)
     for layer in range(layer_dev):
         value = x_ref[layer]
         centered = value - jnp.mean(value, axis=1, keepdims=True)
-        partial_value = jnp.sum(centered * centered)
-        energy = jnp.where(row_layer == layer, partial_value, energy)
+        energy = jnp.where(row == layer, jnp.sum(centered * centered), energy)
         for strip in range(groups * strips):
-            group, part = divmod(strip, strips)
-            out_ref[group, pl.ds(part * rows + layer, tok_dev, stride=layer_dev), :] = centered[
+            rows_ref[pl.ds(strip * rows + layer, tok_dev, stride=layer_dev), :] = centered[
                 :, strip * LANES : (strip + 1) * LANES
             ]
+    first, rest = split(energy)
+    second, rest = split(rest)
+    energy = jnp.where(lane == 0, first.astype(jnp.float32), jnp.where(lane == 1, second.astype(jnp.float32), rest))
     for group in range(groups):
-        out_ref[group, strips * rows :, :] = energy
+        for start in range(0, half, tile):
+            high, rest = split(rows_ref[group * half + start : group * half + start + tile, :])
+            if start == half - tile:
+                rest = jnp.where(slots, energy, rest)
+            out_ref[group, start : start + tile, :] = high
+            out_ref[group, half + start : half + start + tile, :] = rest.astype(jnp.bfloat16)
 
 
-def route_kernel(count, block_rows, owners_ref, x_ref, out_ref):
+def route_kernel(count, layer_dev, block_rows, owners_ref, x_ref, out_ref):
     groups, all_rows, _ = x_ref.shape
     blocks, message_rows, _ = out_ref.shape
     strips = message_rows // block_rows
-    rows = (all_rows - SUBLANES) // strips
+    half = all_rows // 2
+    rows = half // strips
     blocks_dev = blocks // groups
-    energy = x_ref[0, strips * rows :, :]
+    tile = 2 * SUBLANES
+    _, _, slots = energy_slots((tile, LANES), layer_dev)
+    energy = x_ref[0, all_rows - tile :, :].astype(jnp.float32)
     for group in range(1, groups):
-        energy += x_ref[group, strips * rows :, :]
-    scale = 1.0 / jnp.sqrt(energy / count + 1.0)
-    scale = jnp.concatenate([scale] * (block_rows // SUBLANES), axis=0)
+        energy += x_ref[group, all_rows - tile :, :].astype(jnp.float32)
+    energy = jnp.sum(jnp.where(slots, energy, 0.0), axis=1, keepdims=True)
+    scale = 1.0 / jnp.sqrt(energy[:layer_dev] / count + 1.0)
+    scale = jnp.concatenate([scale] * (block_rows // layer_dev), axis=0)
     for group in range(groups):
         for block in range(blocks_dev):
             owner = owners_ref[group * blocks_dev + block]
             for part in range(strips):
-                start = part * rows + block * block_rows
-                value = x_ref[group, start : start + block_rows, :] * scale
-                out_ref[owner, part * block_rows : (part + 1) * block_rows, :] = value.astype(
-                    jnp.bfloat16
-                )
+                for piece in range(0, block_rows, tile):
+                    start = part * rows + block * block_rows + piece
+                    rest = x_ref[group, half + start : half + start + tile, :].astype(jnp.float32)
+                    if start == half - tile:
+                        rest = jnp.where(slots, 0.0, rest)
+                    value = x_ref[group, start : start + tile, :].astype(jnp.float32) + rest
+                    value = value * scale[piece : piece + tile]
+                    place = part * block_rows + piece
+                    out_ref[owner, place : place + tile, :] = value.astype(jnp.bfloat16)
 
 
 def merge_kernel(layer_dev, x_ref, out_ref):
@@ -82,17 +110,19 @@
     blocks = owners.shape[0]
     block_len = tok_dev * groups // blocks
     strips = features // groups // LANES
-    rows = tok_dev * layer_dev
+    half = strips * tok_dev * layer_dev
     block_rows = block_len * layer_dev
     message = pl.pallas_call(
         spread_kernel,
-        out_shape=jax.ShapeDtypeStruct((groups, strips * rows + SUBLANES, LANES), jnp.float32),
+        out_shape=jax.ShapeDtypeStruct((groups, 2 * half, LANES), jnp.bfloat16),
+        scratch_shapes=[pltpu.VMEM((groups * half, LANES), jnp.float32)],
         compiler_params=LOCAL,
         name="spread",
     )(residuals)
     spread = lax.all_to_all(message, "dp", split_axis=0, concat_axis=0, tiled=True)
+    count = float(tok_dev * groups * features)
     routed = pl.pallas_call(
-        lambda *refs: route_kernel(float(tok_dev * groups * features), block_rows, *refs),
+        lambda *refs: route_kernel(count, layer_dev, block_rows, *refs),
         out_shape=jax.ShapeDtypeStruct((blocks, strips * block_rows, LANES), jnp.bfloat16),
         in_specs=[
             pl.BlockSpec(memory_space=pltpu.SMEM),

time: 40.5 us -> 38.9 us (0.960)
  blocking collectives: 37.4 us -> 35.6 us
    all_to_all x1, blocking collectives: 24.4 us -> 21.5 us  [on_device(): lax.all_to_all(message, 'dp', split_axis=0, concat_axis=0, tiled=True)]
    all_to_all x1, blocking collectives: 13 us -> 14.2 us  [on_device(): lax.all_to_all(routed, ('section', 'dp'), split_axis=0, concat_axis=0, ti...]
where the time goes in v3:
time: 38.9 us; the launch traced here: 38.7 us
  blocking collectives  35.6 us (92%)
  Pallas kernels  1.97 us (5%)
  local copies, waits for them, and re-layouts  1.05 us (3%)
    all_to_all x1, blocking collectives, on_device(): lax.all_to_all(message, 'dp', split_axis=0, concat_axis=0, tiled=True)  21.5 us
    all_to_all x1, blocking collectives, on_device(): lax.all_to_all(routed, ('section', 'dp'), split_axis=0, concat_axis=0, ti...  14.2 us
    unnamed x4, local copies, waits for them, and re-layouts  1.05 us
    pallas_call x1, Pallas kernels, on_device(): pl.pallas_call(lambda *refs: merge_kernel(layer_dev, *refs), out_shape=ja...  0.8 us

profile of v3, /device:TPU:0, one launch (start us, length us, event | category | flops | bytes accessed | tf_op | source)
XLA Modules:
  0.0 38.7 jit_solution(3014328890614328925)
XLA Ops:
  0.0 0.0 copy-start
  0.0 1.0 %copy-done = f32[4,8,4096]{2,1,0:T(8,128)S(1)} copy-done((f32[4,8,4096]{2,1,0:T(8,128)S(1)}, f32[4,8,4096]{2,1,0:T(8,128)}, u32[]{:S(2)}) %copy-start) | copy-done | bytes 524312
  1.0 0.4 %spread.1 = bf16[16,128,128]{2,1,0:T(8,128)(2,1)S(1)} custom-call(f32[4,8,4096]{2,1,0:T(8,128)S(1)} %copy-done), custom_call_target="tpu_custom_call" | custom-call | tf_op jit(solution)/shard_map/spread/pallas_call | solution.py:115
  1.5 0.0 copy-start.1
  1.5 21.5 %all_to_all.10.refs_1_ = bf16[16,128,128]{2,1,0:T(8,128)(2,1)S(1)} all-to-all(bf16[16,128,128]{2,1,0:T(8,128)(2,1)S(1)} %spread.1), channel_id=1, replica_groups=mesh['section'=2,'dp'=16] {'dp'}, dimensions={0} | all-to-all | bytes 1048576 | tf_op jit(solution)/shard_map/all_to_all | solution.py:122
  22.9 0.0 copy-done.1
  22.9 0.7 %route.1 = bf16[32,32,128]{2,1,0:T(8,128)(2,1)S(1)} custom-call(s32[32]{0:T(128)S(1)} %copy-done.1, bf16[16,128,128]{2,1,0:T(8,128)(2,1)S(1)} %all_to_all.10.refs_1_), custom_call_target="tpu_custom_call" | custom-call | tf_op jit(solution)/shard_map/route/pallas_call | solution.py:124
  23.7 14.2 %all_to_all.11.refs_0_ = bf16[32,32,128]{2,1,0:T(8,128)(2,1)S(1)} all-to-all(bf16[32,32,128]{2,1,0:T(8,128)(2,1)S(1)} %route.1), channel_id=1, replica_groups=mesh['section'=2,'dp'=16] {'section','dp'}, dimensions={0} | all-to-all | bytes 524288 | tf_op jit(solution)/shard_map/all_to_all | solution.py:134
  37.9 0.8 %merge.1 = bf16[4,8,4096]{2,1,0:T(8,128)(2,1)} custom-call(bf16[32,32,128]{2,1,0:T(8,128)(2,1)S(1)} %all_to_all.11.refs_0_), custom_call_target="tpu_custom_call" | custom-call | tf_op jit(solution)/shard_map/merge/pallas_call | solution.py:135
Async XLA Ops:
  0.0 1.0 %copy-start = (f32[4,8,4096]{2,1,0:T(8,128)S(1)}, f32[4,8,4096]{2,1,0:T(8,128)}, u32[]{:S(2)}) copy-start(f32[4,8,4096]{2,1,0:T(8,128)} %x_ref.1) | copy-start | bytes 1572868
  1.5 21.5 %copy-start.1 = (s32[32]{0:T(128)S(1)}, s32[32]{0:T(128)}, u32[]{:S(2)}) copy-start(s32[32]{0:T(128)} %refs_0_.1) | copy-start | bytes 388

commit v4 on v3

--- a/solution.py
+++ b/solution.py
@@ -9,6 +9,10 @@
 SUBLANES = 8
 PARTS = 3
 LOCAL = pltpu.CompilerParams(vmem_limit_bytes=16 * 1024 * 1024)
+
+
+def ring_order(groups):
+    return [(groups * 3 // 4 - 1 - place) % groups for place in range(groups)]
 
 
 def split(value):
@@ -51,7 +55,7 @@
             out_ref[group, half + start : half + start + tile, :] = rest.astype(jnp.bfloat16)
 
 
-def route_kernel(count, layer_dev, block_rows, owners_ref, x_ref, out_ref):
+def route_kernel(order, count, layer_dev, block_rows, owners_ref, x_ref, out_ref):
     groups, all_rows, _ = x_ref.shape
     blocks, message_rows, _ = out_ref.shape
     strips = message_rows // block_rows
@@ -68,7 +72,7 @@
     scale = jnp.concatenate([scale] * (block_rows // layer_dev), axis=0)
     for group in range(groups):
         for block in range(blocks_dev):
-            owner = owners_ref[group * blocks_dev + block]
+            owner = owners_ref[order[group] * blocks_dev + block]
             for part in range(strips):
                 for piece in range(0, block_rows, tile):
                     start = part * rows + block * block_rows + piece
@@ -81,7 +85,7 @@
                     out_ref[owner, place : place + tile, :] = value.astype(jnp.bfloat16)
 
 
-def merge_kernel(layer_dev, x_ref, out_ref):
+def merge_kernel(order, layer_dev, x_ref, out_ref):
     block_len, layers, features = out_ref.shape
     devices, message_rows, _ = x_ref.shape
     block_rows = block_len * layer_dev
@@ -95,7 +99,7 @@
                 start = part * block_rows + token * layer_dev
                 value = jnp.concatenate(
                     [
-                        x_ref[section * groups + group, start : start + layer_dev, :]
+                        x_ref[section * groups + order[group], start : start + layer_dev, :]
                         for section in range(sections)
                     ],
                     axis=0,
@@ -111,6 +115,7 @@
     block_len = tok_dev * groups // blocks
     strips = features // groups // LANES
     half = strips * tok_dev * layer_dev
+    order = ring_order(groups)
     block_rows = block_len * layer_dev
     message = pl.pallas_call(
         spread_kernel,
@@ -119,10 +124,12 @@
         compiler_params=LOCAL,
         name="spread",
     )(residuals)
-    spread = lax.all_to_all(message, "dp", split_axis=0, concat_axis=0, tiled=True)
+    spread = lax.all_to_all(
+        message, "dp", split_axis=0, concat_axis=0, tiled=True, axis_index_groups=[order]
+    )
     count = float(tok_dev * groups * features)
     routed = pl.pallas_call(
-        lambda *refs: route_kernel(count, layer_dev, block_rows, *refs),
+        lambda *refs: route_kernel(order, count, layer_dev, block_rows, *refs),
         out_shape=jax.ShapeDtypeStruct((blocks, strips * block_rows, LANES), jnp.bfloat16),
         in_specs=[
             pl.BlockSpec(memory_space=pltpu.SMEM),
@@ -133,7 +140,7 @@
     )(owners, spread)
     received = lax.all_to_all(routed, ("section", "dp"), split_axis=0, concat_axis=0, tiled=True)
     return pl.pallas_call(
-        lambda *refs: merge_kernel(layer_dev, *refs),
+        lambda *refs: merge_kernel(order, layer_dev, *refs),
         out_shape=jax.ShapeDtypeStruct((block_len, layer_dev * sections, features), jnp.bfloat16),
         compiler_params=LOCAL,
         name="merge",

time: 38.9 us -> 36.4 us (0.936)
  blocking collectives: 35.6 us -> 33.2 us
    all_to_all x1, blocking collectives: 21.5 us -> 19.4 us  [on_device(): lax.all_to_all(message, 'dp', split_axis=0, concat_axis=0, tiled=True, ax...]
where the time goes in v4:
time: 36.4 us; the launch traced here: 36.2 us
  blocking collectives  33.2 us (91%)
  Pallas kernels  1.97 us (5%)
  local copies, waits for them, and re-layouts  1.05 us (3%)
    all_to_all x1, blocking collectives, on_device(): lax.all_to_all(message, 'dp', split_axis=0, concat_axis=0, tiled=True, ax...  19.4 us
    all_to_all x1, blocking collectives, on_device(): lax.all_to_all(routed, ('section', 'dp'), split_axis=0, concat_axis=0, ti...  13.8 us
    unnamed x4, local copies, waits for them, and re-layouts  1.05 us
    pallas_call x1, Pallas kernels, on_device(): pl.pallas_call(lambda *refs: merge_kernel(order, layer_dev, *refs), out_s...  0.8 us
    pallas_call x1, Pallas kernels, on_device(): pl.pallas_call(lambda *refs: route_kernel(order, count, layer_dev, block_...  0.74 us

profile of v4, /device:TPU:0, one launch (start us, length us, event | category | flops | bytes accessed | tf_op | source)
XLA Modules:
  0.0 36.2 jit_solution(17509006544163890845)
XLA Ops:
  0.0 0.0 copy-start
  0.0 1.0 %copy-done = f32[4,8,4096]{2,1,0:T(8,128)S(1)} copy-done((f32[4,8,4096]{2,1,0:T(8,128)S(1)}, f32[4,8,4096]{2,1,0:T(8,128)}, u32[]{:S(2)}) %copy-start) | copy-done | bytes 524312
  1.0 0.4 %spread.1 = bf16[16,128,128]{2,1,0:T(8,128)(2,1)S(1)} custom-call(f32[4,8,4096]{2,1,0:T(8,128)S(1)} %copy-done), custom_call_target="tpu_custom_call" | custom-call | tf_op jit(solution)/shard_map/spread/pallas_call | solution.py:120
  1.5 0.0 copy-start.1
  1.5 19.4 %all_to_all.10.refs_1_ = bf16[16,128,128]{2,1,0:T(8,128)(2,1)S(1)} all-to-all(bf16[16,128,128]{2,1,0:T(8,128)(2,1)S(1)} %spread.1), channel_id=1, replica_groups={{11,10,9,8,7,6,5,4,3,2,1,0,15,14,13,12},{27,26,25,24,23,22,21,20,19,18,..., dimensions={0} | all-to-all | bytes 1048576 | tf_op jit(solution)/shard_map/all_to_all | solution.py:127
  20.9 0.0 copy-done.1
  20.9 0.7 %route.1 = bf16[32,32,128]{2,1,0:T(8,128)(2,1)S(1)} custom-call(s32[32]{0:T(128)S(1)} %copy-done.1, bf16[16,128,128]{2,1,0:T(8,128)(2,1)S(1)} %all_to_all.10.refs_1_), custom_call_target="tpu_custom_call" | custom-call | tf_op jit(solution)/shard_map/route/pallas_call | solution.py:131
  21.6 13.8 %all_to_all.11.refs_0_ = bf16[32,32,128]{2,1,0:T(8,128)(2,1)S(1)} all-to-all(bf16[32,32,128]{2,1,0:T(8,128)(2,1)S(1)} %route.1), channel_id=1, replica_groups=mesh['section'=2,'dp'=16] {'section','dp'}, dimensions={0} | all-to-all | bytes 524288 | tf_op jit(solution)/shard_map/all_to_all | solution.py:141
  35.4 0.8 %merge.1 = bf16[4,8,4096]{2,1,0:T(8,128)(2,1)} custom-call(bf16[32,32,128]{2,1,0:T(8,128)(2,1)S(1)} %all_to_all.11.refs_0_), custom_call_target="tpu_custom_call" | custom-call | tf_op jit(solution)/shard_map/merge/pallas_call | solution.py:142
Async XLA Ops:
  0.0 1.0 %copy-start = (f32[4,8,4096]{2,1,0:T(8,128)S(1)}, f32[4,8,4096]{2,1,0:T(8,128)}, u32[]{:S(2)}) copy-start(f32[4,8,4096]{2,1,0:T(8,128)} %x_ref.1) | copy-start | bytes 1572868
  1.5 19.4 %copy-start.1 = (s32[32]{0:T(128)S(1)}, s32[32]{0:T(128)}, u32[]{:S(2)}) copy-start(s32[32]{0:T(128)} %refs_0_.1) | copy-start | bytes 388

commit v5 on v4

v5 whole, which is shorter than its diff:
```python
import jax
import jax.numpy as jnp
from jax import lax
from jax.experimental import pallas as pl
from jax.experimental.pallas import tpu as pltpu
from jax.sharding import PartitionSpec as P

LANES = 128
SUBLANES = 8
PARTS = 3
LOCAL = pltpu.CompilerParams(vmem_limit_bytes=16 * 1024 * 1024)


def ring_order(groups):
    return [(groups * 3 // 4 - 1 - place) % groups for place in range(groups)]


def split(value):
    high = value.astype(jnp.bfloat16)
    return high, value - high.astype(jnp.float32)


def energy_slots(high, layer_dev):
    weight = high * high
    weight = weight[:SUBLANES] + weight[SUBLANES:]
    for shift in (4, 2, 1):
        weight += pltpu.roll(weight, shift, 0)
    lane = lax.broadcasted_iota(jnp.int32, weight.shape, 1).astype(jnp.float32)
    least = jnp.min(weight, axis=1, keepdims=True)
    first = jnp.min(jnp.where(weight == least, lane, float(LANES)), axis=1, keepdims=True)
    row = lax.broadcasted_iota(jnp.int32, high.shape, 0)
    chosen = jnp.concatenate([jnp.where(lane == first, 1.0, 0.0)] * 2, axis=0)
    return (chosen > 0.0) & (row < PARTS * layer_dev)


def spread_kernel(x_ref, out_ref, rows_ref):
    layer_dev, tok_dev, features = x_ref.shape
    groups, all_rows, _ = out_ref.shape
    strips = features // groups // LANES
    rows = tok_dev * layer_dev
    half = all_rows // 2
    tile = 2 * SUBLANES
    row = lax.broadcasted_iota(jnp.int32, (tile, LANES), 0)
    energy = jnp.zeros((tile, LANES), jnp.float32)
    for layer in range(layer_dev):
        value = x_ref[layer]
        centered = value - jnp.mean(value, axis=1, keepdims=True)
        energy = jnp.where(row % layer_dev == layer, jnp.sum(centered * centered), energy)
        for strip in range(groups * strips):
            rows_ref[pl.ds(strip * rows + layer, tok_dev, stride=layer_dev), :] = centered[
                :, strip * LANES : (strip + 1) * LANES
            ]
    first, rest = split(energy)
    second, rest = split(rest)
    energy = jnp.where(
        row < layer_dev,
        first.astype(jnp.float32),
        jnp.where(row < 2 * layer_dev, second.astype(jnp.float32), rest),
    )
    for group in range(groups):
        for start in range(0, half, tile):
            high, rest = split(rows_ref[group * half + start : group * half + start + tile, :])
            if start == half - tile:
                slots = energy_slots(high.astype(jnp.float32), layer_dev)
                rest = jnp.where(slots, energy, rest)
            out_ref[group, start : start + tile, :] = high
            out_ref[group, half + start : half + start + tile, :] = rest.astype(jnp.bfloat16)


def route_kernel(place_of, order, count, layer_dev, block_rows, owners_ref, x_ref, out_ref):
    groups, all_rows, _ = x_ref.shape
    blocks, message_rows, _ = out_ref.shape
    owners = owners_ref[...]
    strips = message_rows // block_rows
    half = all_rows // 2
    rows = half // strips
    blocks_dev = blocks // groups
    tile = 2 * SUBLANES
    energy = jnp.zeros((tile, LANES), jnp.float32)
    slots = []
    for group in range(groups):
        slots.append(energy_slots(x_ref[group, half - tile : half, :].astype(jnp.float32), layer_dev))
        rest = x_ref[group, all_rows - tile :, :].astype(jnp.float32)
        energy += jnp.where(slots[group], rest, 0.0)
    energy = jnp.sum(energy, axis=1, keepdims=True)
    energy = sum(energy[part * layer_dev : (part + 1) * layer_dev] for part in range(PARTS))
    scale = 1.0 / jnp.sqrt(energy / count + 1.0)
    scale = jnp.concatenate([scale] * (block_rows // layer_dev), axis=0)
    for group in range(groups):
        for block in range(blocks_dev):
            owner = place_of(owners[order[group] * blocks_dev + block])
            for part in range(strips):
                for piece in range(0, block_rows, tile):
                    start = part * rows + block * block_rows + piece
                    rest = x_ref[group, half + start : half + start + tile, :].astype(jnp.float32)
                    if start == half - tile:
                        rest = jnp.where(slots[group], 0.0, rest)
                    value = x_ref[group, start : start + tile, :].astype(jnp.float32) + rest
                    value = value * scale[piece : piece + tile]
                    place = part * block_rows + piece
                    out_ref[owner, place : place + tile, :] = value.astype(jnp.bfloat16)


def merge_kernel(place_of, order, layer_dev, x_ref, out_ref):
    block_len, layers, features = out_ref.shape
    devices, message_rows, _ = x_ref.shape
    block_rows = block_len * layer_dev
    strips = message_rows // block_rows
    sections = layers // layer_dev
    groups = devices // sections
    for group in range(groups):
        for part in range(strips):
            column = (group * strips + part) * LANES
            for token in range(block_len):
                start = part * block_rows + token * layer_dev
                value = jnp.concatenate(
                    [
                        x_ref[place_of(section * groups + order[group]), start : start + layer_dev, :]
                        for section in range(sections)
                    ],
                    axis=0,
                )
                out_ref[token, :, column : column + LANES] = value


def on_device(residuals, owners):
    layer_dev, tok_dev, features = residuals.shape
    groups = lax.axis_size("dp")
    sections = lax.axis_size("section")
    blocks = owners.shape[0]
    block_len = tok_dev * groups // blocks
    strips = features // groups // LANES
    half = strips * tok_dev * layer_dev
    order = ring_order(groups)

    def place_of(device):
        return (groups - 1 - device % groups) * sections + device // groups

    block_rows = block_len * layer_dev
    message = pl.pallas_call(
        spread_kernel,
        out_shape=jax.ShapeDtypeStruct((groups, 2 * half, LANES), jnp.bfloat16),
        scratch_shapes=[pltpu.VMEM((groups * half, LANES), jnp.float32)],
        compiler_params=LOCAL,
        name="spread",
    )(residuals)
    spread = lax.all_to_all(
        message, "dp", split_axis=0, concat_axis=0, tiled=True, axis_index_groups=[order]
    )
    count = float(tok_dev * groups * features)
    routed = pl.pallas_call(
        lambda *refs: route_kernel(place_of, order, count, layer_dev, block_rows, *refs),
        out_shape=jax.ShapeDtypeStruct((blocks, strips * block_rows, LANES), jnp.bfloat16),
        compiler_params=LOCAL,
        name="route",
    )(owners, spread)
    received = lax.all_to_all(
        routed,
        ("section", "dp"),
        split_axis=0,
        concat_axis=0,
        tiled=True,
        axis_index_groups=[sorted(range(blocks), key=place_of)],
    )
    return pl.pallas_call(
        lambda *refs: merge_kernel(place_of, order, layer_dev, *refs),
        out_shape=jax.ShapeDtypeStruct((block_len, layer_dev * sections, features), jnp.bfloat16),
        compiler_params=LOCAL,
        name="merge",
    )(received)


def solution(mesh):
    in_specs = (P("section", "dp", None), P())
    out_specs = P(("section", "dp"), None, None)
    return jax.shard_map(
        on_device, mesh=mesh, in_specs=in_specs, out_specs=out_specs, check_vma=False
    )
```

time: 36.4 us -> 35.9 us (0.986)
  blocking collectives: 33.2 us -> 32.8 us
    all_to_all x1, blocking collectives: 13.8 us -> 13.3 us  [on_device(): lax.all_to_all(routed, ('section', 'dp'), split_axis=0, concat_axis=0, ti...]
where the time goes in v5:
time: 35.9 us; the launch traced here: 35.7 us
  blocking collectives  32.8 us (91%)
  Pallas kernels  1.82 us (5%)
  local copies, waits for them, and re-layouts  1.04 us (3%)
    all_to_all x1, blocking collectives, on_device(): lax.all_to_all(message, 'dp', split_axis=0, concat_axis=0, tiled=True, ax...  19.5 us
    all_to_all x1, blocking collectives, on_device(): lax.all_to_all(routed, ('section', 'dp'), split_axis=0, concat_axis=0, ti...  13.3 us
    unnamed x4, local copies, waits for them, and re-layouts  1.04 us
    pallas_call x1, Pallas kernels, on_device(): pl.pallas_call(lambda *refs: merge_kernel(place_of, order, layer_dev, *re...  0.81 us

profile of v5, /device:TPU:0, one launch (start us, length us, event | category | flops | bytes accessed | tf_op | source)
XLA Modules:
  0.0 35.7 jit_solution(17631968405718702995)
XLA Ops:
  0.0 0.0 copy-start
  0.0 1.0 %copy-done = f32[4,8,4096]{2,1,0:T(8,128)S(1)} copy-done((f32[4,8,4096]{2,1,0:T(8,128)S(1)}, f32[4,8,4096]{2,1,0:T(8,128)}, u32[]{:S(2)}) %copy-start) | copy-done | bytes 524312
  1.0 0.5 %spread.1 = bf16[16,128,128]{2,1,0:T(8,128)(2,1)S(1)} custom-call(f32[4,8,4096]{2,1,0:T(8,128)S(1)} %copy-done), custom_call_target="tpu_custom_call" | custom-call | tf_op jit(solution)/shard_map/spread/pallas_call | solution.py:140
  1.5 0.0 copy-start.1
  1.5 19.5 %all_to_all.10.refs_1_ = bf16[16,128,128]{2,1,0:T(8,128)(2,1)S(1)} all-to-all(bf16[16,128,128]{2,1,0:T(8,128)(2,1)S(1)} %spread.1), channel_id=1, replica_groups={{11,10,9,8,7,6,5,4,3,2,1,0,15,14,13,12},{27,26,25,24,23,22,21,20,19,18,..., dimensions={0} | all-to-all | bytes 1048576 | tf_op jit(solution)/shard_map/all_to_all | solution.py:147
  21.0 0.0 copy-done.1
  21.1 0.5 %route.1 = bf16[32,32,128]{2,1,0:T(8,128)(2,1)S(1)} custom-call(s32[32]{0:T(128)S(1)} %copy-done.1, bf16[16,128,128]{2,1,0:T(8,128)(2,1)S(1)} %all_to_all.10.refs_1_), custom_call_target="tpu_custom_call" | custom-call | tf_op jit(solution)/shard_map/route/pallas_call | solution.py:151
  21.6 13.3 %all_to_all.11.refs_0_ = bf16[32,32,128]{2,1,0:T(8,128)(2,1)S(1)} all-to-all(bf16[32,32,128]{2,1,0:T(8,128)(2,1)S(1)} %route.1), channel_id=1, replica_groups={{15,31,14,30,13,29,12,28,11,27,10,26,9,25,8,24,7,23,6,22,5,21,4,20,3,19..., dimensions={0} | all-to-all | bytes 524288 | tf_op jit(solution)/shard_map/all_to_all | solution.py:157
  34.9 0.8 %merge.1 = bf16[4,8,4096]{2,1,0:T(8,128)(2,1)} custom-call(bf16[32,32,128]{2,1,0:T(8,128)(2,1)S(1)} %all_to_all.11.refs_0_), custom_call_target="tpu_custom_call" | custom-call | tf_op jit(solution)/shard_map/merge/pallas_call | solution.py:165
Async XLA Ops:
  0.0 1.0 %copy-start = (f32[4,8,4096]{2,1,0:T(8,128)S(1)}, f32[4,8,4096]{2,1,0:T(8,128)}, u32[]{:S(2)}) copy-start(f32[4,8,4096]{2,1,0:T(8,128)} %x_ref.1) | copy-start | bytes 1572868
  1.5 19.5 %copy-start.1 = (s32[32]{0:T(128)S(1)}, s32[32]{0:T(128)}, u32[]{:S(2)}) copy-start(s32[32]{0:T(128)} %refs_0_.1) | copy-start | bytes 388

commit v6 on v5

--- a/solution.py
+++ b/solution.py
@@ -20,17 +20,16 @@
     return high, value - high.astype(jnp.float32)
 
 
-def energy_slots(high, layer_dev):
+def spare_lane(high):
     weight = high * high
     weight = weight[:SUBLANES] + weight[SUBLANES:]
     for shift in (4, 2, 1):
         weight += pltpu.roll(weight, shift, 0)
-    lane = lax.broadcasted_iota(jnp.int32, weight.shape, 1).astype(jnp.float32)
+    lane = lax.broadcasted_iota(jnp.int32, weight.shape, 1)
+    weight = jnp.where(lane == 0, jnp.inf, weight)
     least = jnp.min(weight, axis=1, keepdims=True)
-    first = jnp.min(jnp.where(weight == least, lane, float(LANES)), axis=1, keepdims=True)
-    row = lax.broadcasted_iota(jnp.int32, high.shape, 0)
-    chosen = jnp.concatenate([jnp.where(lane == first, 1.0, 0.0)] * 2, axis=0)
-    return (chosen > 0.0) & (row < PARTS * layer_dev)
+    first = jnp.min(jnp.where(weight == least, lane.astype(jnp.float32), float(LANES)), axis=1, keepdims=True)
+    return jnp.concatenate([first, first], axis=0)
 
 
 def spread_kernel(x_ref, out_ref, rows_ref):
@@ -41,6 +40,8 @@
     half = all_rows // 2
     tile = 2 * SUBLANES
     row = lax.broadcasted_iota(jnp.int32, (tile, LANES), 0)
+    lane = lax.broadcasted_iota(jnp.int32, (tile, LANES), 1)
+    note = PARTS * layer_dev
     energy = jnp.zeros((tile, LANES), jnp.float32)
     for layer in range(layer_dev):
         value = x_ref[layer]
@@ -57,12 +58,19 @@
         first.astype(jnp.float32),
         jnp.where(row < 2 * layer_dev, second.astype(jnp.float32), rest),
     )
+    spares = []
+    for group in range(groups):
+        high, _ = split(rows_ref[(group + 1) * half - tile : (group + 1) * half, :])
+        spares.append(spare_lane(high.astype(jnp.float32)))
     for group in range(groups):
         for start in range(0, half, tile):
             high, rest = split(rows_ref[group * half + start : group * half + start + tile, :])
             if start == half - tile:
-                slots = energy_slots(high.astype(jnp.float32), layer_dev)
-                rest = jnp.where(slots, energy, rest)
+                spare = spares[group]
+                moved = (lane.astype(jnp.float32) == spare) & (row <= note)
+                rest = jnp.where(moved, rest[:, :1], rest)
+                fixed = jnp.where(row < note, energy, jnp.where(row == note, spare, rest))
+                rest = jnp.where(lane == 0, fixed, rest)
             out_ref[group, start : start + tile, :] = high
             out_ref[group, half + start : half + start + tile, :] = rest.astype(jnp.bfloat16)
 
@@ -76,13 +84,18 @@
     rows = half // strips
     blocks_dev = blocks // groups
     tile = 2 * SUBLANES
+    row = lax.broadcasted_iota(jnp.int32, (tile, LANES), 0)
+    lane = lax.broadcasted_iota(jnp.int32, (tile, LANES), 1)
+    note = PARTS * layer_dev
     energy = jnp.zeros((tile, LANES), jnp.float32)
-    slots = []
+    last = []
     for group in range(groups):
-        slots.append(energy_slots(x_ref[group, half - tile : half, :].astype(jnp.float32), layer_dev))
         rest = x_ref[group, all_rows - tile :, :].astype(jnp.float32)
-        energy += jnp.where(slots[group], rest, 0.0)
-    energy = jnp.sum(energy, axis=1, keepdims=True)
+        energy += rest
+        moved = (lane.astype(jnp.float32) == rest[note : note + 1, :1]) & (row <= note)
+        first = jnp.sum(jnp.where(moved, rest, 0.0), axis=1, keepdims=True)
+        last.append(jnp.where(moved, 0.0, jnp.where((lane == 0) & (row <= note), first, rest)))
+    energy = energy[:, :1]
     energy = sum(energy[part * layer_dev : (part + 1) * layer_dev] for part in range(PARTS))
     scale = 1.0 / jnp.sqrt(energy / count + 1.0)
     scale = jnp.concatenate([scale] * (block_rows // layer_dev), axis=0)
@@ -92,9 +105,10 @@
             for part in range(strips):
                 for piece in range(0, block_rows, tile):
                     start = part * rows + block * block_rows + piece
-                    rest = x_ref[group, half + start : half + start + tile, :].astype(jnp.float32)
                     if start == half - tile:
-                        rest = jnp.where(slots[group], 0.0, rest)
+                        rest = last[group]
+                    else:
+                        rest = x_ref[group, half + start : half + start + tile, :].astype(jnp.float32)
                     value = x_ref[group, start : start + tile, :].astype(jnp.float32) + rest
                     value = value * scale[piece : piece + tile]
                     place = part * block_rows + piece

time: 35.9 us -> 35.8 us (level)
  no operation moved by 1% of the time
where the time goes in v6:
time: 35.8 us; the launch traced here: 35.6 us
  blocking collectives  32.8 us (92%)
  Pallas kernels  1.72 us (5%)
  local copies, waits for them, and re-layouts  1.04 us (3%)
    all_to_all x1, blocking collectives, on_device(): lax.all_to_all(message, 'dp', split_axis=0, concat_axis=0, tiled=True, ax...  19.5 us
    all_to_all x1, blocking collectives, on_device(): lax.all_to_all(routed, ('section', 'dp'), split_axis=0, concat_axis=0, ti...  13.3 us
    unnamed x4, local copies, waits for them, and re-layouts  1.04 us
    pallas_call x1, Pallas kernels, on_device(): pl.pallas_call(lambda *refs: merge_kernel(place_of, order, layer_dev, *re...  0.81 us

profile of v6, /device:TPU:0, one launch (start us, length us, event | category | flops | bytes accessed | tf_op | source)
XLA Modules:
  0.0 35.6 jit_solution(10475383210195880990)
XLA Ops:
  0.0 0.0 copy-start
  0.0 1.0 %copy-done = f32[4,8,4096]{2,1,0:T(8,128)S(1)} copy-done((f32[4,8,4096]{2,1,0:T(8,128)S(1)}, f32[4,8,4096]{2,1,0:T(8,128)}, u32[]{:S(2)}) %copy-start) | copy-done | bytes 524312
  1.0 0.6 %spread.1 = bf16[16,128,128]{2,1,0:T(8,128)(2,1)S(1)} custom-call(f32[4,8,4096]{2,1,0:T(8,128)S(1)} %copy-done), custom_call_target="tpu_custom_call" | custom-call | tf_op jit(solution)/shard_map/spread/pallas_call | solution.py:154
  1.6 0.0 copy-start.1
  1.6 19.5 %all_to_all.10.refs_1_ = bf16[16,128,128]{2,1,0:T(8,128)(2,1)S(1)} all-to-all(bf16[16,128,128]{2,1,0:T(8,128)(2,1)S(1)} %spread.1), channel_id=1, replica_groups={{11,10,9,8,7,6,5,4,3,2,1,0,15,14,13,12},{27,26,25,24,23,22,21,20,19,18,..., dimensions={0} | all-to-all | bytes 1048576 | tf_op jit(solution)/shard_map/all_to_all | solution.py:161
  21.1 0.0 copy-done.1
  21.1 0.3 route.1
  21.5 13.3 %all_to_all.11.refs_0_ = bf16[32,32,128]{2,1,0:T(8,128)(2,1)S(1)} all-to-all(bf16[32,32,128]{2,1,0:T(8,128)(2,1)S(1)} %route.1), channel_id=1, replica_groups={{15,31,14,30,13,29,12,28,11,27,10,26,9,25,8,24,7,23,6,22,5,21,4,20,3,19..., dimensions={0} | all-to-all | bytes 524288 | tf_op jit(solution)/shard_map/all_to_all | solution.py:171
  34.8 0.8 %merge.1 = bf16[4,8,4096]{2,1,0:T(8,128)(2,1)} custom-call(bf16[32,32,128]{2,1,0:T(8,128)(2,1)S(1)} %all_to_all.11.refs_0_), custom_call_target="tpu_custom_call" | custom-call | tf_op jit(solution)/shard_map/merge/pallas_call | solution.py:179
Async XLA Ops:
  0.0 1.0 %copy-start = (f32[4,8,4096]{2,1,0:T(8,128)S(1)}, f32[4,8,4096]{2,1,0:T(8,128)}, u32[]{:S(2)}) copy-start(f32[4,8,4096]{2,1,0:T(8,128)} %x_ref.1) | copy-start | bytes 1572868
  1.6 19.5 %copy-start.1 = (s32[32]{0:T(128)S(1)}, s32[32]{0:T(128)}, u32[]{:S(2)}) copy-start(s32[32]{0:T(128)} %refs_0_.1) | copy-start | bytes 388

commit v7 on v6

--- a/solution.py
+++ b/solution.py
@@ -20,8 +20,7 @@
     return high, value - high.astype(jnp.float32)
 
 
-def spare_lane(high):
-    weight = high * high
+def spare_lane(weight):
     weight = weight[:SUBLANES] + weight[SUBLANES:]
     for shift in (4, 2, 1):
         weight += pltpu.roll(weight, shift, 0)
@@ -58,19 +57,19 @@
         first.astype(jnp.float32),
         jnp.where(row < 2 * layer_dev, second.astype(jnp.float32), rest),
     )
-    spares = []
+    weight = jnp.zeros((tile, LANES), jnp.float32)
     for group in range(groups):
-        high, _ = split(rows_ref[(group + 1) * half - tile : (group + 1) * half, :])
-        spares.append(spare_lane(high.astype(jnp.float32)))
+        value = rows_ref[(group + 1) * half - tile : (group + 1) * half, :]
+        weight += value * value
+    spare = spare_lane(weight)
+    moved = (lane.astype(jnp.float32) == spare) & (row <= note)
+    noted = jnp.where(row < note, energy, spare)
     for group in range(groups):
         for start in range(0, half, tile):
             high, rest = split(rows_ref[group * half + start : group * half + start + tile, :])
             if start == half - tile:
-                spare = spares[group]
-                moved = (lane.astype(jnp.float32) == spare) & (row <= note)
                 rest = jnp.where(moved, rest[:, :1], rest)
-                fixed = jnp.where(row < note, energy, jnp.where(row == note, spare, rest))
-                rest = jnp.where(lane == 0, fixed, rest)
+                rest = jnp.where((lane == 0) & (row <= note), noted, rest)
             out_ref[group, start : start + tile, :] = high
             out_ref[group, half + start : half + start + tile, :] = rest.astype(jnp.bfloat16)
 

time: 35.8 us -> 35.6 us (level)
  no operation moved by 1% of the time
where the time goes in v7:
time: 35.6 us; the launch traced here: 35.4 us
  blocking collectives  32.7 us (92%)
  Pallas kernels  1.64 us (5%)
  local copies, waits for them, and re-layouts  1.05 us (3%)
    all_to_all x1, blocking collectives, on_device(): lax.all_to_all(message, 'dp', split_axis=0, concat_axis=0, tiled=True, ax...  19.4 us
    all_to_all x1, blocking collectives, on_device(): lax.all_to_all(routed, ('section', 'dp'), split_axis=0, concat_axis=0, ti...  13.3 us
    unnamed x4, local copies, waits for them, and re-layouts  1.05 us
    pallas_call x1, Pallas kernels, on_device(): pl.pallas_call(lambda *refs: merge_kernel(place_of, order, layer_dev, *re...  0.81 us

profile of v7, /device:TPU:0, one launch (start us, length us, event | category | flops | bytes accessed | tf_op | source)
XLA Modules:
  0.0 35.4 jit_solution(3716820681559707728)
XLA Ops:
  0.0 0.0 copy-start
  0.0 1.0 %copy-done = f32[4,8,4096]{2,1,0:T(8,128)S(1)} copy-done((f32[4,8,4096]{2,1,0:T(8,128)S(1)}, f32[4,8,4096]{2,1,0:T(8,128)}, u32[]{:S(2)}) %copy-start) | copy-done | bytes 524312
  1.0 0.5 %spread.1 = bf16[16,128,128]{2,1,0:T(8,128)(2,1)S(1)} custom-call(f32[4,8,4096]{2,1,0:T(8,128)S(1)} %copy-done), custom_call_target="tpu_custom_call" | custom-call | tf_op jit(solution)/shard_map/spread/pallas_call | solution.py:153
  1.6 0.0 copy-start.1
  1.6 19.4 %all_to_all.10.refs_1_ = bf16[16,128,128]{2,1,0:T(8,128)(2,1)S(1)} all-to-all(bf16[16,128,128]{2,1,0:T(8,128)(2,1)S(1)} %spread.1), channel_id=1, replica_groups={{11,10,9,8,7,6,5,4,3,2,1,0,15,14,13,12},{27,26,25,24,23,22,21,20,19,18,..., dimensions={0} | all-to-all | bytes 1048576 | tf_op jit(solution)/shard_map/all_to_all | solution.py:160
  20.9 0.0 copy-done.1
  20.9 0.3 route.1
  21.3 13.3 %all_to_all.11.refs_0_ = bf16[32,32,128]{2,1,0:T(8,128)(2,1)S(1)} all-to-all(bf16[32,32,128]{2,1,0:T(8,128)(2,1)S(1)} %route.1), channel_id=1, replica_groups={{15,31,14,30,13,29,12,28,11,27,10,26,9,25,8,24,7,23,6,22,5,21,4,20,3,19..., dimensions={0} | all-to-all | bytes 524288 | tf_op jit(solution)/shard_map/all_to_all | solution.py:170
  34.6 0.8 %merge.1 = bf16[4,8,4096]{2,1,0:T(8,128)(2,1)} custom-call(bf16[32,32,128]{2,1,0:T(8,128)(2,1)S(1)} %all_to_all.11.refs_0_), custom_call_target="tpu_custom_call" | custom-call | tf_op jit(solution)/shard_map/merge/pallas_call | solution.py:178
Async XLA Ops:
  0.0 1.0 %copy-start = (f32[4,8,4096]{2,1,0:T(8,128)S(1)}, f32[4,8,4096]{2,1,0:T(8,128)}, u32[]{:S(2)}) copy-start(f32[4,8,4096]{2,1,0:T(8,128)} %x_ref.1) | copy-start | bytes 1572868
  1.6 19.4 %copy-start.1 = (s32[32]{0:T(128)S(1)}, s32[32]{0:T(128)}, u32[]{:S(2)}) copy-start(s32[32]{0:T(128)} %refs_0_.1) | copy-start | bytes 388

commit v8 on v7

--- a/solution.py
+++ b/solution.py
@@ -114,17 +114,18 @@
                     out_ref[owner, place : place + tile, :] = value.astype(jnp.bfloat16)
 
 
-def merge_kernel(place_of, order, layer_dev, x_ref, out_ref):
+def merge_kernel(place_of, order, layer_dev, x_ref, out_ref, near_ref, sems):
     block_len, layers, features = out_ref.shape
     devices, message_rows, _ = x_ref.shape
     block_rows = block_len * layer_dev
     strips = message_rows // block_rows
     sections = layers // layer_dev
     groups = devices // sections
-    for group in range(groups):
-        for part in range(strips):
-            column = (group * strips + part) * LANES
-            for token in range(block_len):
+    stores = []
+    for token in range(block_len):
+        for group in range(groups):
+            for part in range(strips):
+                column = (group * strips + part) * LANES
                 start = part * block_rows + token * layer_dev
                 value = jnp.concatenate(
                     [
@@ -133,7 +134,12 @@
                     ],
                     axis=0,
                 )
-                out_ref[token, :, column : column + LANES] = value
+                near_ref[token, :, column : column + LANES] = value
+        store = pltpu.make_async_copy(near_ref.at[token], out_ref.at[token], sems.at[token])
+        store.start()
+        stores.append(store)
+    for store in stores:
+        store.wait()
 
 
 def on_device(residuals, owners):
@@ -147,7 +153,8 @@
     order = ring_order(groups)
 
     def place_of(device):
-        return (groups - 1 - device % groups) * sections + device // groups
+        index = device % groups
+        return (index ^ 3 if groups % 4 == 0 else index) * sections + device // groups
 
     block_rows = block_len * layer_dev
     message = pl.pallas_call(
@@ -178,6 +185,11 @@
     return pl.pallas_call(
         lambda *refs: merge_kernel(place_of, order, layer_dev, *refs),
         out_shape=jax.ShapeDtypeStruct((block_len, layer_dev * sections, features), jnp.bfloat16),
+        out_specs=pl.BlockSpec(memory_space=pltpu.HBM),
+        scratch_shapes=[
+            pltpu.VMEM((block_len, layer_dev * sections, features), jnp.bfloat16),
+            pltpu.SemaphoreType.DMA((block_len,)),
+        ],
         compiler_params=LOCAL,
         name="merge",
     )(received)

time: 35.6 us -> 35.5 us (level)
  no operation moved by 1% of the time
where the time goes in v8:
time: 35.5 us; the launch traced here: 35.3 us
  blocking collectives  32.6 us (92%)
  Pallas kernels  1.61 us (5%)
  local copies, waits for them, and re-layouts  1.05 us (3%)
    all_to_all x1, blocking collectives, on_device(): lax.all_to_all(message, 'dp', split_axis=0, concat_axis=0, tiled=True, ax...  19.4 us
    all_to_all x1, blocking collectives, on_device(): lax.all_to_all(routed, ('section', 'dp'), split_axis=0, concat_axis=0, ti...  13.2 us
    unnamed x4, local copies, waits for them, and re-layouts  1.05 us
    pallas_call x1, Pallas kernels, on_device(): pl.pallas_call(lambda *refs: merge_kernel(place_of, order, layer_dev, *re...  0.77 us

profile of v8, /device:TPU:0, one launch (start us, length us, event | category | flops | bytes accessed | tf_op | source)
XLA Modules:
  0.0 35.3 jit_solution(14350715819341113037)
XLA Ops:
  0.0 0.0 copy-start
  0.0 1.0 %copy-done = f32[4,8,4096]{2,1,0:T(8,128)S(1)} copy-done((f32[4,8,4096]{2,1,0:T(8,128)S(1)}, f32[4,8,4096]{2,1,0:T(8,128)}, u32[]{:S(2)}) %copy-start) | copy-done | bytes 524312
  1.0 0.5 %spread.1 = bf16[16,128,128]{2,1,0:T(8,128)(2,1)S(1)} custom-call(f32[4,8,4096]{2,1,0:T(8,128)S(1)} %copy-done), custom_call_target="tpu_custom_call" | custom-call | tf_op jit(solution)/shard_map/spread/pallas_call | solution.py:160
  1.6 0.0 copy-start.1
  1.6 19.4 %all_to_all.10.refs_1_ = bf16[16,128,128]{2,1,0:T(8,128)(2,1)S(1)} all-to-all(bf16[16,128,128]{2,1,0:T(8,128)(2,1)S(1)} %spread.1), channel_id=1, replica_groups={{11,10,9,8,7,6,5,4,3,2,1,0,15,14,13,12},{27,26,25,24,23,22,21,20,19,18,..., dimensions={0} | all-to-all | bytes 1048576 | tf_op jit(solution)/shard_map/all_to_all | solution.py:167
  20.9 0.0 copy-done.1
  20.9 0.3 route.1
  21.3 13.2 %all_to_all.11.refs_0_ = bf16[32,32,128]{2,1,0:T(8,128)(2,1)S(1)} all-to-all(bf16[32,32,128]{2,1,0:T(8,128)(2,1)S(1)} %route.1), channel_id=1, replica_groups={{3,19,2,18,1,17,0,16,7,23,6,22,5,21,4,20,11,27,10,26,9,25,8,24,15,31,14..., dimensions={0} | all-to-all | bytes 524288 | tf_op jit(solution)/shard_map/all_to_all | solution.py:177
  34.5 0.8 %merge.1 = bf16[4,8,4096]{2,1,0:T(8,128)(2,1)} custom-call(bf16[32,32,128]{2,1,0:T(8,128)(2,1)S(1)} %all_to_all.11.refs_0_), custom_call_target="tpu_custom_call" | custom-call | tf_op jit(solution)/shard_map/merge/pallas_call | solution.py:185
Async XLA Ops:
  0.0 1.0 %copy-start = (f32[4,8,4096]{2,1,0:T(8,128)S(1)}, f32[4,8,4096]{2,1,0:T(8,128)}, u32[]{:S(2)}) copy-start(f32[4,8,4096]{2,1,0:T(8,128)} %x_ref.1) | copy-start | bytes 1572868
  1.6 19.4 %copy-start.1 = (s32[32]{0:T(128)S(1)}, s32[32]{0:T(128)}, u32[]{:S(2)}) copy-start(s32[32]{0:T(128)} %refs_0_.1) | copy-start | bytes 388

commit v9 on v8

--- a/solution.py
+++ b/solution.py
@@ -26,8 +26,7 @@
         weight += pltpu.roll(weight, shift, 0)
     lane = lax.broadcasted_iota(jnp.int32, weight.shape, 1)
     weight = jnp.where(lane == 0, jnp.inf, weight)
-    least = jnp.min(weight, axis=1, keepdims=True)
-    first = jnp.min(jnp.where(weight == least, lane.astype(jnp.float32), float(LANES)), axis=1, keepdims=True)
+    first = jnp.argmin(weight, axis=1, keepdims=True).astype(jnp.float32)
     return jnp.concatenate([first, first], axis=0)
 
 

time: 35.5 us -> 35.4 us (level)
  no operation moved by 1% of the time
where the time goes in v9:
time: 35.4 us; the launch traced here: 35.2 us
  blocking collectives  32.6 us (92%)
  Pallas kernels  1.56 us (4%)
  local copies, waits for them, and re-layouts  1.05 us (3%)
    all_to_all x1, blocking collectives, on_device(): lax.all_to_all(message, 'dp', split_axis=0, concat_axis=0, tiled=True, ax...  19.4 us
    all_to_all x1, blocking collectives, on_device(): lax.all_to_all(routed, ('section', 'dp'), split_axis=0, concat_axis=0, ti...  13.2 us
    unnamed x4, local copies, waits for them, and re-layouts  1.05 us
    pallas_call x1, Pallas kernels, on_device(): pl.pallas_call(lambda *refs: merge_kernel(place_of, order, layer_dev, *re...  0.77 us

profile of v9, /device:TPU:0, one launch (start us, length us, event | category | flops | bytes accessed | tf_op | source)
XLA Modules:
  0.0 35.2 jit_solution(12518870307326280527)
XLA Ops:
  0.0 0.0 copy-start
  0.0 1.0 %copy-done = f32[4,8,4096]{2,1,0:T(8,128)S(1)} copy-done((f32[4,8,4096]{2,1,0:T(8,128)S(1)}, f32[4,8,4096]{2,1,0:T(8,128)}, u32[]{:S(2)}) %copy-start) | copy-done | bytes 524312
  1.0 0.5 %spread.1 = bf16[16,128,128]{2,1,0:T(8,128)(2,1)S(1)} custom-call(f32[4,8,4096]{2,1,0:T(8,128)S(1)} %copy-done), custom_call_target="tpu_custom_call" | custom-call | tf_op jit(solution)/shard_map/spread/pallas_call | solution.py:159
  1.5 0.0 copy-start.1
  1.5 19.4 %all_to_all.10.refs_1_ = bf16[16,128,128]{2,1,0:T(8,128)(2,1)S(1)} all-to-all(bf16[16,128,128]{2,1,0:T(8,128)(2,1)S(1)} %spread.1), channel_id=1, replica_groups={{11,10,9,8,7,6,5,4,3,2,1,0,15,14,13,12},{27,26,25,24,23,22,21,20,19,18,..., dimensions={0} | all-to-all | bytes 1048576 | tf_op jit(solution)/shard_map/all_to_all | solution.py:166
  20.9 0.0 copy-done.1
  20.9 0.3 route.1
  21.2 13.2 %all_to_all.11.refs_0_ = bf16[32,32,128]{2,1,0:T(8,128)(2,1)S(1)} all-to-all(bf16[32,32,128]{2,1,0:T(8,128)(2,1)S(1)} %route.1), channel_id=1, replica_groups={{3,19,2,18,1,17,0,16,7,23,6,22,5,21,4,20,11,27,10,26,9,25,8,24,15,31,14..., dimensions={0} | all-to-all | bytes 524288 | tf_op jit(solution)/shard_map/all_to_all | solution.py:176
  34.4 0.8 %merge.1 = bf16[4,8,4096]{2,1,0:T(8,128)(2,1)} custom-call(bf16[32,32,128]{2,1,0:T(8,128)(2,1)S(1)} %all_to_all.11.refs_0_), custom_call_target="tpu_custom_call" | custom-call | tf_op jit(solution)/shard_map/merge/pallas_call | solution.py:184
Async XLA Ops:
  0.0 1.0 %copy-start = (f32[4,8,4096]{2,1,0:T(8,128)S(1)}, f32[4,8,4096]{2,1,0:T(8,128)}, u32[]{:S(2)}) copy-start(f32[4,8,4096]{2,1,0:T(8,128)} %x_ref.1) | copy-start | bytes 1572868
  1.5 19.4 %copy-start.1 = (s32[32]{0:T(128)S(1)}, s32[32]{0:T(128)}, u32[]{:S(2)}) copy-start(s32[32]{0:T(128)} %refs_0_.1) | copy-start | bytes 388

commit v10 on v9

--- a/solution.py
+++ b/solution.py
@@ -153,7 +153,7 @@
 
     def place_of(device):
         index = device % groups
-        return (index ^ 3 if groups % 4 == 0 else index) * sections + device // groups
+        return (groups - 1 - index) * sections + device // groups
 
     block_rows = block_len * layer_dev
     message = pl.pallas_call(

time: 35.4 us -> 35.5 us (level)
  no operation moved by 1% of the time
where the time goes in v10:
time: 35.5 us; the launch traced here: 35.3 us
  blocking collectives  32.7 us (92%)
  Pallas kernels  1.56 us (4%)
  local copies, waits for them, and re-layouts  1.05 us (3%)
    all_to_all x1, blocking collectives, on_device(): lax.all_to_all(message, 'dp', split_axis=0, concat_axis=0, tiled=True, ax...  19.4 us
    all_to_all x1, blocking collectives, on_device(): lax.all_to_all(routed, ('section', 'dp'), split_axis=0, concat_axis=0, ti...  13.3 us
    unnamed x4, local copies, waits for them, and re-layouts  1.05 us
    pallas_call x1, Pallas kernels, on_device(): pl.pallas_call(lambda *refs: merge_kernel(place_of, order, layer_dev, *re...  0.77 us

profile of v10, /device:TPU:0, one launch (start us, length us, event | category | flops | bytes accessed | tf_op | source)
XLA Modules:
  0.0 35.3 jit_solution(696814593950369144)
XLA Ops:
  0.0 0.0 copy-start
  0.0 1.0 %copy-done = f32[4,8,4096]{2,1,0:T(8,128)S(1)} copy-done((f32[4,8,4096]{2,1,0:T(8,128)S(1)}, f32[4,8,4096]{2,1,0:T(8,128)}, u32[]{:S(2)}) %copy-start) | copy-done | bytes 524312
  1.0 0.5 %spread.1 = bf16[16,128,128]{2,1,0:T(8,128)(2,1)S(1)} custom-call(f32[4,8,4096]{2,1,0:T(8,128)S(1)} %copy-done), custom_call_target="tpu_custom_call" | custom-call | tf_op jit(solution)/shard_map/spread/pallas_call | solution.py:159
  1.5 0.0 copy-start.1
  1.5 19.4 %all_to_all.10.refs_1_ = bf16[16,128,128]{2,1,0:T(8,128)(2,1)S(1)} all-to-all(bf16[16,128,128]{2,1,0:T(8,128)(2,1)S(1)} %spread.1), channel_id=1, replica_groups={{11,10,9,8,7,6,5,4,3,2,1,0,15,14,13,12},{27,26,25,24,23,22,21,20,19,18,..., dimensions={0} | all-to-all | bytes 1048576 | tf_op jit(solution)/shard_map/all_to_all | solution.py:166
  20.9 0.0 copy-done.1
  20.9 0.3 route.1
  21.2 13.3 %all_to_all.11.refs_0_ = bf16[32,32,128]{2,1,0:T(8,128)(2,1)S(1)} all-to-all(bf16[32,32,128]{2,1,0:T(8,128)(2,1)S(1)} %route.1), channel_id=1, replica_groups={{15,31,14,30,13,29,12,28,11,27,10,26,9,25,8,24,7,23,6,22,5,21,4,20,3,19..., dimensions={0} | all-to-all | bytes 524288 | tf_op jit(solution)/shard_map/all_to_all | solution.py:176
  34.5 0.8 %merge.1 = bf16[4,8,4096]{2,1,0:T(8,128)(2,1)} custom-call(bf16[32,32,128]{2,1,0:T(8,128)(2,1)S(1)} %all_to_all.11.refs_0_), custom_call_target="tpu_custom_call" | custom-call | tf_op jit(solution)/shard_map/merge/pallas_call | solution.py:184
Async XLA Ops:
  0.0 1.0 %copy-start = (f32[4,8,4096]{2,1,0:T(8,128)S(1)}, f32[4,8,4096]{2,1,0:T(8,128)}, u32[]{:S(2)}) copy-start(f32[4,8,4096]{2,1,0:T(8,128)} %x_ref.1) | copy-start | bytes 1572868
  1.5 19.4 %copy-start.1 = (s32[32]{0:T(128)S(1)}, s32[32]{0:T(128)}, u32[]{:S(2)}) copy-start(s32[32]{0:T(128)} %refs_0_.1) | copy-start | bytes 388
